TPU v7x, 1024 devices: a whole 4x8x16 slice. The times are simulated.
1024 devices in a mesh: row: 16 (over z_hi, x), col: 64 (over z_lo, y, core).
Axes of the slice: x: 4, y: 8, z: 16 (z_hi: 4, z_lo: 4; z = z_hi * 4 + z_lo), core: 2. Of those that a mesh axis runs over, the one named last changes fastest.
Arguments:
- queries: bfloat16 [64, 2048, 1024], P('col', 'row'), may hold values from -120 to 120
- keys: bfloat16 [64, 2048, 128], P('col', 'row'), may hold values from -8 to 8
- values: bfloat16 [64, 2048, 128], P('col', 'row'), may hold values from -6 to 6
- outputs: bfloat16 [64, 2048, 1024], P('col', 'row'), may hold values from -6 to 6
- out_grad: bfloat16 [64, 2048, 1024], P('col', 'row'), may hold values from -192 to 192
- positions: int32 [64, 2048], P('col'), may hold values from 0 to 2047, each once within a row
- tile_flags: int32 [64, 16, 16], P('col', 'row'), may hold values 0 or 1
Outputs:
- query_grad: bfloat16 [64, 2048, 1024], P('col', 'row')
- key_grad: bfloat16 [64, 2048, 128], P('col', 'row')
- value_grad: bfloat16 [64, 2048, 128], P('col', 'row')
All inputs are finite; a program needn't handle non-finite values. No bound on the sum of `tile_flags` on one device may be relied on, other than what follows from the above.
Results may differ from a plain program's by a relative error of at most 0.0065.
Values may be sent and summed in bfloat16 or wider, within the bound.
A program may use at most 64 MiB of HBM per device.

v0:
```python
import math

import jax
import jax.numpy as jnp
from jax import lax
from jax.sharding import PartitionSpec as P

H = 8
HD = 128


def sent_together(arrays, axis, dim, along):
    widths = [a.shape[along] for a in arrays]
    both = jnp.concatenate(arrays, axis=along)
    result = lax.all_gather(both, axis, axis=dim, tiled=True)
    return tuple(jnp.split(result, [sum(widths[:k]) for k in range(1, len(widths))], axis=along))


def side_by_side(arrays, axis, dim, along):
    ends, at = ([], 0)
    for a in arrays[:-1]:
        at += a.shape[along]
        ends.append(at)
    both = jnp.concatenate(arrays, axis=along)
    return tuple(
        jnp.split(lax.psum_scatter(both, axis, scatter_dimension=dim, tiled=True), ends, axis=along)
    )


def combine_stats(left_pair, right_pair):
    larger = jnp.maximum(left_pair[0], right_pair[0])
    total = left_pair[1] * jnp.exp(left_pair[0] - larger) + right_pair[1] * jnp.exp(
        right_pair[0] - larger
    )
    return (larger, total)


def body(queries, keys, values, outputs, out_grad, positions, tile_flags):
    score_scale = 1.0 / math.sqrt(HD)
    row_at = lax.axis_index("row")
    key_all, value_all = sent_together((keys, values), "row", 1, 0)
    key_rows = key_all[0]
    value_rows = value_all[0]
    tokens = queries.shape[1]
    length = key_rows.shape[0]
    shards = length // tokens
    query_heads = queries[0].reshape(tokens, H, HD)
    grad_heads = out_grad[0].reshape(tokens, H, HD)
    output_heads = outputs[0].reshape(tokens, H, HD)
    trace_pos = positions[0]
    flag_row = tile_flags[0, 0]
    query_index = row_at * tokens + jnp.arange(tokens, dtype=jnp.int32)
    query_pos = lax.dynamic_slice_in_dim(trace_pos, row_at * tokens, tokens)
    blocks = length // tokens

    def block_allowed(start):
        key_index = start + jnp.arange(tokens, dtype=jnp.int32)
        key_pos = lax.dynamic_slice_in_dim(trace_pos, start, tokens)
        owner = key_index // tokens
        match = owner[:, None] == jnp.arange(shards, dtype=jnp.int32)[None, :]
        key_flag = jnp.sum(jnp.where(match, flag_row[None, :], 0), axis=1)
        return (key_pos[None, :] <= query_pos[:, None]) & (
            (key_flag[None, :] == 1) | (key_index[None, :] == query_index[:, None])
        )

    def block_scores(start):
        key_piece = lax.dynamic_slice_in_dim(key_rows, start, tokens, 0)
        return (
            jnp.einsum("qhd,kd->hqk", query_heads, key_piece, preferred_element_type=jnp.float32)
            * score_scale
        )

    def stats_step(step, carry):
        start = (step * tokens).astype(jnp.int32)
        allowed = block_allowed(start)
        masked = jnp.where(allowed[None], block_scores(start), -1e30)
        local_max = jnp.max(masked, axis=2)
        local_sum = jnp.sum(
            jnp.where(allowed[None], jnp.exp(masked - local_max[:, :, None]), 0.0), axis=2
        )
        return combine_stats(carry, (local_max, local_sum))

    start_stats = (jnp.full((H, tokens), -1e30, jnp.float32), jnp.zeros((H, tokens), jnp.float32))
    row_max, row_sum = lax.fori_loop(0, blocks, stats_step, start_stats)
    log_total = row_max + jnp.log(row_sum)
    out_dot = jnp.sum(grad_heads.astype(jnp.float32) * output_heads.astype(jnp.float32), axis=2).T

    def grad_step(step, buffers):
        start = (step * tokens).astype(jnp.int32)
        allowed = block_allowed(start)
        grad_buffer, weight_buffer = buffers
        weights = jnp.where(
            allowed[None], jnp.exp(block_scores(start) - log_total[:, :, None]), 0.0
        )
        value_piece = lax.dynamic_slice_in_dim(value_rows, start, tokens, 0)
        grad_probs = jnp.einsum(
            "qhd,kd->hqk", grad_heads, value_piece, preferred_element_type=jnp.float32
        )
        grad_scores = (weights * (grad_probs - out_dot[:, :, None]) * score_scale).astype(
            jnp.bfloat16
        )
        weights_low = weights.astype(jnp.bfloat16)
        grad_buffer = lax.dynamic_update_slice_in_dim(grad_buffer, grad_scores, start, 2)
        weight_buffer = lax.dynamic_update_slice_in_dim(weight_buffer, weights_low, start, 2)
        return (grad_buffer, weight_buffer)

    empty = jnp.zeros((H, tokens, length), jnp.bfloat16)
    grad_scores, weights_low = lax.fori_loop(0, blocks, grad_step, (empty, empty))
    query_grad = jnp.einsum(
        "hqk,kd->qhd", grad_scores, key_rows, preferred_element_type=jnp.float32
    )
    query_grad = query_grad.reshape(1, tokens, H * HD).astype(jnp.bfloat16)
    key_part = jnp.einsum(
        "hqk,qhd->kd", grad_scores, query_heads, preferred_element_type=jnp.float32
    )
    value_part = jnp.einsum(
        "hqk,qhd->kd", weights_low, grad_heads, preferred_element_type=jnp.float32
    )
    key_grad, value_grad = side_by_side((key_part, value_part), "row", 0, 1)
    return (query_grad, key_grad[None].astype(jnp.bfloat16), value_grad[None].astype(jnp.bfloat16))


def solution(mesh):
    placed = (
        P("col", "row", None),
        P("col", "row", None),
        P("col", "row", None),
        P("col", "row", None),
        P("col", "row", None),
        P("col", None),
        P("col", "row", None),
    )
    return jax.shard_map(
        body,
        mesh=mesh,
        in_specs=placed,
        out_specs=(P("col", "row", None), P("col", "row", None), P("col", "row", None)),
        check_vma=False,
    )
```

profile of v0, /device:TPU:8, one launch (start us, length us, event | category | flops | bytes accessed | tf_op | source)
XLA Modules:
  0.0 327.4 jit_solution(12416214730180419433)
XLA Ops:
  9.7 1.1 copy.42
  11.0 1.1 copy.46
  12.2 1.1 copy.45
  14.2 93.5 %all-gather.2.cloned.1.call-done = bf16[2,2048,128]{1,2,0:T(8,128)(2,1)} async-done(((bf16[2,128,128]{1,2,0:T(8,128)(2,1)}), bf16[2,2048,128]{1,2,0:T(8,128)(2,1)}) %all-gather.2.cloned.1.call-update) | async-done | bytes 1048592 | tf_op jit(solution)/shard_map/all_gather | solution.py:15
  107.7 1.3 slice_bitcast_fusion
  109.2 22.5 %while.37 = (s32[]{:T(128)}, f32[8,128]{1,0:T(8,128)S(1)}, f32[8,128]{1,0:T(8,128)S(1)}, s32[2048]{0:T(1024)}, s32[128]{0:T(128)S(1)}, /*index=5*/s32[1,1,16]{2,...) while((s32[]{:T(128)}, f32[8,128]{1,0:T(8,128)S(1)}, ...), condition=%wide.region_4.5_spmd.clone, body=%wide.region_0.4_spmd.clone.sunk | while | flops 34420868 | bytes 1436173 | solution.py:84
  131.8 2.5 broadcast_in_dim.214.clone
  134.3 2.5 broadcast_in_dim.214
  136.7 48.3 %while.36 = (s32[]{:T(128)}, bf16[8,128,2048]{1,2,0:T(8,128)(2,1)}, bf16[8,128,2048]{1,2,0:T(8,128)(2,1)}, s32[2048]{0:T(1024)}, s32[128]{0:T(128)S(1)}, /*index...) while((s32[]{:T(128)}, bf16[8,128,2048]{1,2,0:T(8,128)(2,1)}, ...), condition=%wide.region_8.9_spmd.clone, body=%wide.region_6.8_spmd.clone.sunk | while | flops 68231296 | bytes 2212375 | solution.py:108
  137.7 1.0 convert_dynamic-update-slice_fusion.2
  140.7 1.0 convert_dynamic-update-slice_fusion.2
  146.7 1.0 convert_dynamic-update-slice_fusion.2
  152.8 1.0 convert_dynamic-update-slice_fusion.2
  155.8 1.0 convert_dynamic-update-slice_fusion.2
  156.8 1.0 fusion.47
  158.8 1.0 convert_dynamic-update-slice_fusion.2
  159.9 1.0 fusion.47
  161.9 1.0 convert_dynamic-update-slice_fusion.2
  162.9 1.0 fusion.47
  164.9 1.1 convert_dynamic-update-slice_fusion.2
  166.0 1.0 fusion.47
  168.0 1.0 convert_dynamic-update-slice_fusion.2
  171.0 1.0 convert_dynamic-update-slice_fusion.2
  174.0 1.0 convert_dynamic-update-slice_fusion.2
  177.0 1.1 convert_dynamic-update-slice_fusion.2
  180.0 1.1 convert_dynamic-update-slice_fusion.2
  181.1 1.0 fusion.47
  185.1 3.8 %convolution_bitcast_fusion.1 = f32[2048,128]{0,1:T(8,128)S(1)} fusion(bf16[8,128,2048]{1,2,0:T(8,128)(2,1)} %get-tuple-element.538, bf16[128,8,128]{0,2,1:T(8,128)(2,1)S(1)} %bitcast.94), kind=kOutput, calls=%fused_computation.50 | convolution fusion | flops 536870912 | bytes 5505024 | tf_op jit(solution)/shard_map/hqk,qhd->kd/dot_general | solution.py:116
  188.9 1.5 convolution_bitcast_fusion.2
  190.4 1.6 pad_maximum_fusion
  192.0 2.9 convolution_convert_fusion
  195.8 122.4 %reduce-scatter.2.cloned.1.call-done = f32[128,256]{0,1:T(8,128)} async-done(((f32[2048,256]{0,1:T(8,128)}), f32[128,256]{0,1:T(8,128)}) %reduce-scatter.2.cloned.1.call-update) | async-done | bytes 131088 | tf_op jit(solution)/shard_map/reduce_scatter | solution.py:26
  (280 shorter events, 58.6 us)
Async XLA Ops:
  7.2 102.1 %copy-start.2 = (s32[1,1,16]{2,1,0:T(1,128)S(1)}, s32[1,1,16]{2,1,0:T(1,128)}, u32[]{:S(2)}) copy-start(s32[1,1,16]{2,1,0:T(1,128)} %param.17) | copy-start | bytes 196
  7.2 100.5 %all-gather.2.cloned.1.call-start = ((), (), s32[]{:S(2)}) async-start(), calls=%async_computation.1 | async-start | bytes 1114112 | tf_op jit(solution)/shard_map/all_gather | solution.py:15
  9.6 308.5 %reduce-scatter.2.cloned.1.call-start = ((), (), s32[]{:S(2)}) async-start(), calls=%async_computation.2 | async-start | bytes 2228224 | tf_op jit(solution)/shard_map/reduce_scatter | solution.py:26
  185.1 3.8 %copy-start = (bf16[8,128,2048]{1,2,0:T(8,128)(2,1)S(1)}, bf16[8,128,2048]{1,2,0:T(8,128)(2,1)}, u32[]{:S(2)}) copy-start(bf16[8,128,2048]{1,2,0:T(8,128)(2,1)} %get-tuple-element.537) | copy-start | bytes 12582916
  190.4 1.6 copy-start.1
Sparse Core Ops, SparseCore 0:
  12.7 94.9 all-gather.1
  192.1 126.0 reduce-scatter.1
where the time goes:
time: 329 us; the launch traced here: 327 us
  waiting for transfers between devices  216 us (66%)
  matrix products  44.5 us (14%)
  local copies, waits for them, and re-layouts  39.3 us (12%)
  between operations  14.2 us (4%)
  other arithmetic  12.5 us (4%)
    reduce_scatter x1, waiting for transfers between devices, side_by_side(): lax.psum_scatter(both, axis, scatter_dimension=dim, tiled=True)  122 us
    all_gather x1, waiting for transfers between devices, sent_together(): result = lax.all_gather(both, axis, axis=dim, tiled=True)  93.5 us
    dynamic_slice x32, local copies, waits for them, and re-layouts, block_allowed(): key_pos = lax.dynamic_slice_in_dim(trace_pos, start, tokens)  24.4 us
    dot_general x32, matrix products, block_scores(): jnp.einsum('qhd,kd->hqk', query_heads, key_piece, preferred_element_type=...  20.3 us
    dot_general x16, matrix products, grad_step(): jnp.einsum('qhd,kd->hqk', grad_heads, value_piece, preferred_element_type...  16 us
    unnamed x17, local copies, waits for them, and re-layouts  8.04 us
  transfers between devices with their start and end apart: 2, of which 2 were waited for; matrix products, arithmetic and copies ran while one was open for 3% of the time, Pallas kernels for 0%

commit v1 on v0

v1 whole, which is shorter than its diff:
```python
import functools
import math

import jax
import jax.numpy as jnp
from jax import lax
from jax.experimental import pallas as pl
from jax.experimental.pallas import tpu as pltpu
from jax.sharding import PartitionSpec as P

H = 8
HD = 128
T = 128
R = 4
HT = H * T
CH = 256
NEG = -1e30
SCALE = 1.0 / math.sqrt(HD)
LOG2E = math.log2(math.e)
NT = (((1,), (1,)), ((), ()))
F32 = jnp.float32
BF16 = jnp.bfloat16
GROUPS = (2, 1, 3, 0)


def kernel(
    q_hbm, k_hbm, v_hbm, o_hbm, g_hbm, pos_ref, flag_ref,
    dq_hbm, dk_ref, dv_ref,
    q_in, o_in, g_in, qs, gs, kv, kt, pos_rows, bias, sbuf, dsbuf,
    top, total, lse, dot_row, pf, tx, xrl, xin, xsum, ztx, zrl, zin, dq_out,
    in_sem, out_sem, gather_send, gather_recv, sum_send, sum_recv,
):
    me = lax.axis_index("row")
    zh = me // R
    x = me % R
    z_dev = {1: ((zh + 1) % R) * R + x, -1: ((zh + R - 1) % R) * R + x}
    x_dev = {1: zh * R + (x + 1) % R, -1: zh * R + (x + R - 1) % R}

    k_copy = pltpu.make_async_copy(k_hbm.at[0], kv.at[0, 0, 0], in_sem.at[0])
    v_copy = pltpu.make_async_copy(v_hbm.at[0], kv.at[0, 0, 1], in_sem.at[1])
    g_copy = pltpu.make_async_copy(g_hbm.at[0], g_in, in_sem.at[2])
    o_copy = pltpu.make_async_copy(o_hbm.at[0], o_in, in_sem.at[3])
    q_copy = pltpu.make_async_copy(q_hbm.at[0], q_in, in_sem.at[4])
    for copy in (k_copy, v_copy, q_copy, g_copy, o_copy):
        copy.start()

    barrier = pltpu.get_barrier_semaphore()
    for dev in (x_dev[1], x_dev[-1], z_dev[1], z_dev[-1]):
        pl.semaphore_signal(
            barrier, inc=1, device_id={"row": dev}, device_id_type=pl.DeviceIdType.MESH
        )

    sent = []

    def remote(src, dst, send, recv, dev):
        copy = pltpu.make_async_remote_copy(
            src_ref=src, dst_ref=dst, send_sem=send, recv_sem=recv,
            device_id={"row": dev}, device_id_type=pl.DeviceIdType.MESH,
        )
        copy.start()
        sent.append(copy)
        return copy

    incoming = {}

    def give(rz, rx, kind, to_rz, to_rx, dev):
        incoming[to_rz, to_rx, kind] = remote(
            kv.at[rz, rx, kind], kv.at[to_rz, to_rx, kind],
            gather_send.at[to_rz, to_rx, kind], gather_recv.at[to_rz, to_rx, kind], dev,
        )

    def got(*slot):
        incoming[slot].wait_recv()

    def along_x(rz):
        give(rz, 0, 0, rz, 3, x_dev[1])
        give(rz, 0, 1, rz, 1, x_dev[-1])
        give(rz, 0, 1, rz, 3, x_dev[1])
        give(rz, 0, 0, rz, 1, x_dev[-1])

    def onward_x(rz):
        got(rz, 3, 0)
        give(rz, 3, 0, rz, 2, x_dev[1])
        got(rz, 1, 1)
        give(rz, 1, 1, rz, 2, x_dev[-1])

    def rest_x(rz):
        got(rz, 3, 1)
        got(rz, 1, 0)
        got(rz, 2, 0)
        got(rz, 2, 1)

    pos_rows[...] = jnp.zeros_like(pos_rows)
    for slot in range(R * R):
        block = ((zh + slot // R) % R) * R + (x + slot % R) % R
        row = pos_ref[:, pl.ds(pl.multiple_of(block * T, T), T)]
        pos_rows[slot : slot + 1, :] = row.astype(F32)

    k_copy.wait()
    v_copy.wait()
    pl.semaphore_wait(barrier, 4)

    give(0, 0, 0, 3, 0, z_dev[1])
    give(0, 0, 1, 1, 0, z_dev[-1])
    give(0, 0, 1, 3, 0, z_dev[1])
    give(0, 0, 0, 1, 0, z_dev[-1])
    along_x(0)

    pos_cols = pos_rows[...].T
    own_pos = pos_rows[0:1, :]
    for slot in range(R * R):
        block = ((zh + slot // R) % R) * R + (x + slot % R) % R
        off = (flag_ref[0, 0, block] - 1).astype(F32) * (-NEG)
        column = jnp.broadcast_to(pos_cols[:, slot : slot + 1], (T, T))
        value = jnp.where(column <= own_pos, 0.0, NEG) + off
        if slot == 0:
            keys_at = lax.broadcasted_iota(jnp.int32, (T, T), 0)
            queries_at = lax.broadcasted_iota(jnp.int32, (T, T), 1)
            value = jnp.where(keys_at == queries_at, 0.0, value)
        bias[slot] = value

    q_copy.wait()
    for h in range(H):
        qs[h * T : (h + 1) * T, :] = q_in[:, h * HD : (h + 1) * HD]
    g_copy.wait()
    o_copy.wait()
    for h in range(H):
        cols = slice(h * HD, (h + 1) * HD)
        gs[h * T : (h + 1) * T, :] = g_in[:, cols]
        product = g_in[:, cols].astype(F32) * o_in[:, cols].astype(F32)
        dot_row[:, h * T : (h + 1) * T] = jnp.sum(product.T, axis=0, keepdims=True)

    top[...] = jnp.full_like(top, NEG)
    total[...] = jnp.zeros_like(total)

    def score_block(rz, rx):
        slot = rz * R + rx
        key_block = kv[rz, rx, 0]
        kt[slot] = key_block.T
        mask = bias[slot]
        mask = jnp.concatenate([mask] * (CH // T), axis=1)
        for c in range(HT // CH):
            part = slice(c * CH, (c + 1) * CH)
            raw = lax.dot_general(key_block, qs[part, :], NT, preferred_element_type=F32)
            score = raw * (SCALE * LOG2E) + mask
            sbuf[slot, :, part] = score
            parts = score.reshape(T // 8, 8, CH)
            old = top[:, part]
            new = jnp.maximum(old, jnp.max(parts, axis=0))
            added = jnp.sum(jnp.exp2(parts - new[None]), axis=0)
            total[:, part] = total[:, part] * jnp.exp2(old - new) + added
            top[:, part] = new

    def score_group(rz):
        def step(rx, carry):
            score_block(rz, rx)
            return carry

        lax.fori_loop(0, R, step, 0)

    onward_x(0)
    got(3, 0, 0)
    give(3, 0, 0, 2, 0, z_dev[1])
    got(1, 0, 1)
    give(1, 0, 1, 2, 0, z_dev[-1])
    got(3, 0, 1)
    along_x(3)
    got(1, 0, 0)
    along_x(1)
    rest_x(0)
    score_group(0)
    onward_x(3)
    onward_x(1)
    got(2, 0, 0)
    got(2, 0, 1)
    along_x(2)
    rest_x(3)
    score_group(3)
    rest_x(1)
    score_group(1)
    onward_x(2)
    rest_x(2)
    score_group(2)

    top_all = jnp.max(top[...], axis=0, keepdims=True)
    total_all = jnp.sum(total[...] * jnp.exp2(top[...] - top_all), axis=0, keepdims=True)
    lse[...] = top_all + jnp.log(total_all) * LOG2E

    def grad_block(rz, rx):
        slot = rz * R + rx
        value_block = kv[rz, rx, 1]
        dk = jnp.zeros((T, HD), F32)
        dv = jnp.zeros((T, HD), F32)
        for c in range(HT // CH):
            part = slice(c * CH, (c + 1) * CH)
            weights = jnp.exp2(sbuf[slot, :, part] - lse[:, part])
            probs = lax.dot_general(value_block, gs[part, :], NT, preferred_element_type=F32)
            grads = (weights * (probs - dot_row[:, part]) * SCALE).astype(BF16)
            dsbuf[slot, :, part] = grads
            dk = dk + jnp.dot(grads, qs[part, :], preferred_element_type=F32)
            dv = dv + jnp.dot(weights.astype(BF16), gs[part, :], preferred_element_type=F32)
        pf[rz, rx, 0] = dk
        pf[rz, rx, 1] = dv
        tx[rz, rx, 0] = dk.astype(BF16)
        tx[rz, rx, 1] = dv.astype(BF16)

    def grad_group(rz):
        def step(rx, carry):
            grad_block(rz, rx)
            return carry

        lax.fori_loop(0, R, step, 0)

    sums = {}

    def give_sum(group, what, src, dst, dev):
        sums[group, what] = remote(
            src, dst, sum_send.at[group, what], sum_recv.at[group, what], dev
        )

    def x_first(rz):
        give_sum(rz, 0, tx.at[rz, 2, 0], xrl.at[rz, 0], x_dev[1])
        give_sum(rz, 1, tx.at[rz, 2, 1], xrl.at[rz, 1], x_dev[-1])
        give_sum(rz, 2, tx.at[rz, 1, 1], xin.at[rz, 0, 1], x_dev[1])
        give_sum(rz, 3, tx.at[rz, 3, 0], xin.at[rz, 1, 0], x_dev[-1])

    def x_second(rz):
        sums[rz, 0].wait_recv()
        tx[rz, 1, 0] = (pf[rz, 1, 0] + xrl[rz, 0].astype(F32)).astype(BF16)
        give_sum(rz, 4, tx.at[rz, 1, 0], xin.at[rz, 0, 0], x_dev[1])
        sums[rz, 1].wait_recv()
        tx[rz, 3, 1] = (pf[rz, 3, 1] + xrl[rz, 1].astype(F32)).astype(BF16)
        give_sum(rz, 5, tx.at[rz, 3, 1], xin.at[rz, 1, 1], x_dev[-1])

    def x_sum(rz):
        for what in (2, 3, 4, 5):
            sums[rz, what].wait_recv()
        for kind in range(2):
            both = xin[rz, 0, kind].astype(F32) + xin[rz, 1, kind].astype(F32)
            xsum[rz, kind] = pf[rz, 0, kind] + both

    def to_z(rz, kind):
        ztx[rz, kind] = xsum[rz, kind].astype(BF16)

    grad_group(2)
    x_first(2)
    grad_group(1)
    x_first(1)
    x_second(2)
    grad_group(3)
    x_first(3)
    x_second(1)
    x_sum(2)
    to_z(2, 0)
    give_sum(R, 0, ztx.at[2, 0], zrl.at[0], z_dev[1])
    to_z(2, 1)
    give_sum(R, 1, ztx.at[2, 1], zrl.at[1], z_dev[-1])
    grad_group(0)
    x_first(0)
    x_second(3)
    x_sum(1)
    to_z(1, 1)
    give_sum(R, 2, ztx.at[1, 1], zin.at[0, 1], z_dev[1])
    x_second(0)
    x_sum(3)
    to_z(3, 0)
    give_sum(R, 3, ztx.at[3, 0], zin.at[1, 0], z_dev[-1])

    for c in range(HT // CH):
        grad_t = jnp.zeros((HD, CH), F32)
        for slot in range(0, R * R):
            grad_t = grad_t + jnp.dot(
                kt[slot], dsbuf[slot, :, c * CH : (c + 1) * CH], preferred_element_type=F32
            )
        for part in range(CH // T):
            h = c * (CH // T) + part
            head = grad_t[:, part * T : (part + 1) * T]
            dq_out[:, h * HD : (h + 1) * HD] = head.T.astype(BF16)
    dq_copy = pltpu.make_async_copy(dq_out, dq_hbm.at[0], out_sem.at[0])
    dq_copy.start()

    sums[R, 0].wait_recv()
    ztx[1, 0] = (xsum[1, 0] + zrl[0].astype(F32)).astype(BF16)
    give_sum(R, 4, ztx.at[1, 0], zin.at[0, 0], z_dev[1])
    sums[R, 1].wait_recv()
    ztx[3, 1] = (xsum[3, 1] + zrl[1].astype(F32)).astype(BF16)
    give_sum(R, 5, ztx.at[3, 1], zin.at[1, 1], z_dev[-1])
    x_sum(0)
    for what in (2, 3, 4, 5):
        sums[R, what].wait_recv()
    for kind, out in ((0, dk_ref), (1, dv_ref)):
        both = zin[0, kind].astype(F32) + zin[1, kind].astype(F32)
        out[0] = (xsum[0, kind] + both).astype(BF16)

    for copy in sent:
        copy.wait_send()
    dq_copy.wait()


def body(queries, keys, values, outputs, out_grad, positions, tile_flags):
    block = jax.ShapeDtypeStruct((1, T, HD), BF16)
    hbm = pl.BlockSpec(memory_space=pl.ANY)
    vmem = pl.BlockSpec(memory_space=pltpu.VMEM)
    dma = pltpu.SemaphoreType.DMA
    return pl.pallas_call(
        kernel,
        out_shape=(jax.ShapeDtypeStruct((1, T, H * HD), BF16), block, block),
        in_specs=[hbm] * 5 + [vmem, pl.BlockSpec(memory_space=pltpu.SMEM)],
        out_specs=(hbm, vmem, vmem),
        scratch_shapes=[
            pltpu.VMEM((T, H * HD), BF16),
            pltpu.VMEM((T, H * HD), BF16),
            pltpu.VMEM((T, H * HD), BF16),
            pltpu.VMEM((HT, HD), BF16),
            pltpu.VMEM((HT, HD), BF16),
            pltpu.VMEM((R, R, 2, T, HD), BF16),
            pltpu.VMEM((R * R, HD, T), BF16),
            pltpu.VMEM((T, T), F32),
            pltpu.VMEM((R * R, T, T), F32),
            pltpu.VMEM((R * R, T, HT), F32),
            pltpu.VMEM((R * R, T, HT), BF16),
            pltpu.VMEM((8, HT), F32),
            pltpu.VMEM((8, HT), F32),
            pltpu.VMEM((1, HT), F32),
            pltpu.VMEM((1, HT), F32),
            pltpu.VMEM((R, R, 2, T, HD), F32),
            pltpu.VMEM((R, R, 2, T, HD), BF16),
            pltpu.VMEM((R, 2, T, HD), BF16),
            pltpu.VMEM((R, 2, 2, T, HD), BF16),
            pltpu.VMEM((R, 2, T, HD), F32),
            pltpu.VMEM((R, 2, T, HD), BF16),
            pltpu.VMEM((2, T, HD), BF16),
            pltpu.VMEM((2, 2, T, HD), BF16),
            pltpu.VMEM((T, H * HD), BF16),
            dma((5,)),
            dma((1,)),
            dma((R, R, 2)),
            dma((R, R, 2)),
            dma((R + 1, 6)),
            dma((R + 1, 6)),
        ],
        compiler_params=pltpu.CompilerParams(
            collective_id=0, has_side_effects=True, vmem_limit_bytes=56 * 1024 * 1024
        ),
        name="attention_backward",
    )(queries, keys, values, outputs, out_grad, positions, tile_flags)


def solution(mesh):
    sharded = P("col", "row", None)
    placed = (sharded,) * 5 + (P("col", None), sharded)
    return jax.shard_map(
        body, mesh=mesh, in_specs=placed, out_specs=(sharded,) * 3, check_vma=False
    )
```

time: 329 us -> 70.6 us (0.21)
  the two profiles are of different devices: /device:TPU:8 before, /device:TPU:72 now
where the time goes in v1:
time: 70.6 us; the launch traced here: 70.3 us
  Pallas kernels  66.6 us (94%)
  local copies, waits for them, and re-layouts  3.06 us (4%)
    pallas_call x1, Pallas kernels, body(): pl.pallas_call(kernel, out_shape=(jax.ShapeDtypeStruct((1, T, H * HD), BF...  66.6 us
    unnamed x7, local copies, waits for them, and re-layouts  3.06 us

profile of v1, /device:TPU:72, one launch (start us, length us, event | category | flops | bytes accessed | tf_op | source)
XLA Modules:
  0.0 70.3 jit_solution(12703399270603378762)
XLA Ops:
  0.6 66.6 %attention_backward.1 = (bf16[1,128,1024]{2,1,0:T(8,128)(2,1)}, bf16[1,128,128]{2,1,0:T(8,128)(2,1)}, bf16[1,128,128]{2,1,0:T(8,128)(2,1)}) custom-call(bf16[1,128,1024]{2,1,0:T(8,128)(2,1)} %q_hbm.1, bf16[1,128,128]{2,1,0:T(8,128)(2,1)} %k_hbm.1, bf16[1,128,128]{2,1,0:T(8,128)(2,1)} %v_hbm.1, bf16[1,128,1024]{2,1,0:T(8,128)(2,1)} %o_hbm.1, ...), custom_call_target="tpu_custom_call" | custom-call | tf_op jit(solution)/shard_map/attention_backward/pallas_call | solution.py:305
  67.2 0.0 copy-start.1
  67.2 1.7 %copy.13 = bf16[1,128,1024]{2,1,0:T(8,128)(2,1)} copy(bf16[1,128,1024]{2,1,0:T(8,128)(2,1)} %get-tuple-element.6) | data formatting | bytes 524288
  68.9 0.0 copy-done.1
  68.9 0.0 copy-start
  68.9 0.6 copy.14
  69.5 0.2 copy-done
  69.7 0.6 copy.15
Async XLA Ops:
  67.2 1.7 %copy-start.1 = (bf16[1,128,128]{2,1,0:T(8,128)(2,1)S(1)}, bf16[1,128,128]{2,1,0:T(8,128)(2,1)}, u32[]{:S(2)}) copy-start(bf16[1,128,128]{2,1,0:T(8,128)(2,1)} %get-tuple-element.7) | copy-start | bytes 98308
  68.9 0.8 %copy-start = (bf16[1,128,128]{2,1,0:T(8,128)(2,1)S(1)}, bf16[1,128,128]{2,1,0:T(8,128)(2,1)}, u32[]{:S(2)}) copy-start(bf16[1,128,128]{2,1,0:T(8,128)(2,1)} %get-tuple-element.8) | copy-start | bytes 98308

commit v2 on v1

v2 whole, which is shorter than its diff:
```python
import math

import jax
import jax.numpy as jnp
from jax import lax
from jax.experimental import pallas as pl
from jax.experimental.pallas import tpu as pltpu
from jax.sharding import PartitionSpec as P

H = 8
HD = 128
T = 128
R = 4
HT = H * T
CH = 256
NEG = -1e30
SCALE = 1.0 / math.sqrt(HD)
LOG2E = math.log2(math.e)
F32 = jnp.float32
BF16 = jnp.bfloat16
RX = (2, 1, 3, 0)
PLACE = {rx: place for place, rx in enumerate(RX)}
HALF = T // 2


def kernel(
    q_hbm, k_hbm, v_hbm, o_hbm, g_hbm, pos_hbm, flag_hbm,
    dq_hbm, dk_ref, dv_ref,
    q_in, o_in, g_in, pos_ref, flag_ref, qs, gs, q_cols, g_cols, kv, kt, pos_rows, bias, sbuf, dsbuf,
    top, total, lse, dot_row, pf, tx, xrl, xin, xsum, ztx, zrl, zin, dq_out,
    in_sem, out_sem, gather_send, gather_recv, x_send, x_recv, z_send, z_recv,
):
    me = lax.axis_index("row")
    zh = me // R
    x = me % R
    z_dev = {1: ((zh + 1) % R) * R + x, -1: ((zh + R - 1) % R) * R + x}
    x_dev = {1: zh * R + (x + 1) % R, 2: zh * R + (x + 2) % R, -1: zh * R + (x + R - 1) % R}

    own = PLACE[0]
    k_copy = pltpu.make_async_copy(k_hbm.at[0], kv.at[0, 0, own], in_sem.at[0])
    v_copy = pltpu.make_async_copy(v_hbm.at[0], kv.at[1, 0, own], in_sem.at[1])
    g_copy = pltpu.make_async_copy(g_hbm.at[0], g_in, in_sem.at[2])
    o_copy = pltpu.make_async_copy(o_hbm.at[0], o_in, in_sem.at[3])
    q_copy = pltpu.make_async_copy(q_hbm.at[0], q_in, in_sem.at[4])
    pos_copy = pltpu.make_async_copy(pos_hbm, pos_ref, in_sem.at[5])
    flag_copy = pltpu.make_async_copy(flag_hbm, flag_ref, in_sem.at[6])
    for copy in (k_copy, v_copy, pos_copy, flag_copy, q_copy, g_copy, o_copy):
        copy.start()

    barrier = pltpu.get_barrier_semaphore()
    for dev in (z_dev[1], z_dev[-1], x_dev[1], x_dev[2], x_dev[-1]):
        pl.semaphore_signal(
            barrier, inc=1, device_id={"row": dev}, device_id_type=pl.DeviceIdType.MESH
        )

    sent = []

    def remote(src, dst, send, recv, dev):
        copy = pltpu.make_async_remote_copy(
            src_ref=src, dst_ref=dst, send_sem=send, recv_sem=recv,
            device_id={"row": dev}, device_id_type=pl.DeviceIdType.MESH,
        )
        copy.start()
        sent.append(copy)
        return copy

    late = []

    def drain(copies):
        while copies:
            copies.pop().wait_send()

    incoming = {}

    def give(kind, src, dst, dev, halves=(None,)):
        (rz, rx), (to_rz, to_rx) = src, dst
        at, to = PLACE[rx], PLACE[to_rx]
        for half in halves:
            rows = pl.ds(0, T) if half is None else pl.ds(half * HALF, HALF)
            incoming.setdefault((kind, dst), []).append(
                remote(
                    kv.at[kind, rz, at, rows, :], kv.at[kind, to_rz, to, rows, :],
                    gather_send.at[kind, half or 0, to_rz, to],
                    gather_recv.at[kind, half or 0, to_rz, to], dev,
                )
            )

    def got(kind, slot):
        for copy in incoming.pop((kind, slot), ()):
            copy.wait_recv()

    def along_z():
        give(0, (0, 0), (3, 0), z_dev[1], (0, 1))
        give(1, (0, 0), (1, 0), z_dev[-1], (0, 1))
        give(1, (0, 0), (3, 0), z_dev[1])
        give(0, (0, 0), (1, 0), z_dev[-1])

    def onward_z():
        for half in range(2):
            for kind, slot, dev in ((0, (3, 0), z_dev[1]), (1, (1, 0), z_dev[-1])):
                incoming[kind, slot].pop(0).wait_recv()
                give(kind, slot, (2, 0), dev, (half,))

    def along_x(rz):
        give(0, (rz, 0), (rz, 3), x_dev[1])
        give(1, (rz, 0), (rz, 1), x_dev[-1])
        give(1, (rz, 0), (rz, 3), x_dev[1])
        give(0, (rz, 0), (rz, 1), x_dev[-1])

    def onward_x(rz, kinds=(0, 1)):
        for kind in kinds:
            slot = (rz, 1 if kind else 3)
            got(kind, slot)
            give(kind, slot, (rz, 2), x_dev[-1 if kind else 1])

    def all_of(kind, rz):
        for rx in range(R):
            got(kind, (rz, rx))

    def block_of(rz, place):
        return ((zh + rz) % R) * R + (x + RX[place]) % R

    slots = [(rz, place) for rz in range(R) for place in range(R)]
    k_copy.wait()
    v_copy.wait()
    pl.semaphore_wait(barrier, 5)

    along_z()
    along_x(0)

    pos_copy.wait()
    flag_copy.wait()
    pos_rows[...] = jnp.zeros_like(pos_rows)
    for i, slot in enumerate(slots):
        row = pos_ref[:, pl.ds(pl.multiple_of(block_of(*slot) * T, T), T)]
        pos_rows[i : i + 1, :] = row.astype(F32)
    pos_cols = pos_rows[...].T
    for i, (rz, place) in enumerate(slots):
        own_pos = pos_rows[own : own + 1, :]
        off = (flag_ref[0, 0, block_of(rz, place)] - 1).astype(F32) * (-NEG)
        column = jnp.broadcast_to(pos_cols[:, i : i + 1], (T, T))
        value = jnp.where(column <= own_pos, 0.0, NEG) + off
        if (rz, place) == (0, own):
            keys_at = lax.broadcasted_iota(jnp.int32, (T, T), 0)
            queries_at = lax.broadcasted_iota(jnp.int32, (T, T), 1)
            value = jnp.where(keys_at == queries_at, 0.0, value)
        bias[rz, place] = value

    q_copy.wait()
    for h in range(H):
        head = q_in[:, h * HD : (h + 1) * HD]
        qs[h * T : (h + 1) * T, :] = head
        q_cols[:, h * T : (h + 1) * T] = head.T
    g_copy.wait()
    o_copy.wait()
    for h in range(H):
        cols = slice(h * HD, (h + 1) * HD)
        head = g_in[:, cols]
        gs[h * T : (h + 1) * T, :] = head
        g_cols[:, h * T : (h + 1) * T] = head.T
        product = head.astype(F32) * o_in[:, cols].astype(F32)
        dot_row[:, h * T : (h + 1) * T] = jnp.sum(product.T, axis=0, keepdims=True)

    top[...] = jnp.full_like(top, NEG)
    total[...] = jnp.zeros_like(total)

    def pair_of(p):
        return pl.ds(2 * p, 2)

    def score_pair(rz, p):
        pair = pair_of(p)
        keys_2 = kv[0, rz, pair].reshape(2 * T, HD)
        kt[rz, p] = keys_2.T
        mask = bias[rz, pair].reshape(2 * T, T)
        mask = jnp.concatenate([mask] * (CH // T), axis=1)
        for c in range(HT // CH):
            part = slice(c * CH, (c + 1) * CH)
            raw = jnp.dot(keys_2, q_cols[:, part], preferred_element_type=F32)
            score = raw * (SCALE * LOG2E) + mask
            sbuf[rz, pair, :, part] = score.reshape(2, T, CH)
            parts = score.reshape(2 * T // 8, 8, CH)
            old = top[:, part]
            new = jnp.maximum(old, jnp.max(parts, axis=0))
            added = jnp.sum(jnp.exp2(parts - new[None]), axis=0)
            total[:, part] = total[:, part] * jnp.exp2(old - new) + added
            top[:, part] = new

    def score_group(rz):
        def step(p, carry):
            score_pair(rz, p)
            return carry

        lax.fori_loop(0, 2, step, 0)

    onward_x(0)
    onward_z()
    got(1, (3, 0))
    along_x(3)
    got(0, (1, 0))
    along_x(1)
    all_of(0, 0)
    score_group(0)
    onward_x(3)
    onward_x(1)
    all_of(0, 3)
    score_group(3)
    got(0, (2, 0))
    give(0, (2, 0), (2, 2), x_dev[2])
    give(0, (2, 0), (2, 3), x_dev[1])
    give(0, (2, 0), (2, 1), x_dev[-1])
    got(1, (2, 0))
    give(1, (2, 0), (2, 1), x_dev[-1])
    give(1, (2, 0), (2, 3), x_dev[1])
    all_of(0, 1)
    score_group(1)
    onward_x(2, (1,))
    got(0, (2, 3))
    score_pair(2, 1)
    all_of(0, 2)
    score_pair(2, 0)

    top_all = jnp.max(top[...], axis=0, keepdims=True)
    total_all = jnp.sum(total[...] * jnp.exp2(top[...] - top_all), axis=0, keepdims=True)
    lse[...] = top_all + jnp.log(total_all) * LOG2E
    for rz in (2, 1, 3, 0):
        all_of(1, rz)

    def grad_pair(rz, p):
        pair = pair_of(p)
        values_2 = kv[1, rz, pair].reshape(2 * T, HD)
        dk = dv = None
        for c in range(HT // CH):
            part = slice(c * CH, (c + 1) * CH)
            probs = jnp.dot(values_2, g_cols[:, part], preferred_element_type=F32)
            weights = jnp.exp2(sbuf[rz, pair, :, part].reshape(2 * T, CH) - lse[:, part])
            grads = (weights * (probs - dot_row[:, part]) * SCALE).astype(BF16)
            dsbuf[rz, pair, :, part] = grads.reshape(2, T, CH)
            dk_c = jnp.dot(grads, qs[part, :], preferred_element_type=F32)
            dv_c = jnp.dot(weights.astype(BF16), gs[part, :], preferred_element_type=F32)
            dk = dk_c if c == 0 else dk + dk_c
            dv = dv_c if c == 0 else dv + dv_c
        for kind, grad in ((0, dk), (1, dv)):
            grad = grad.reshape(2, T, HD)
            pf[kind, rz, pair] = grad
            tx[kind, rz, pair] = grad.astype(BF16)

    sums = {}

    def give_x(rz, what, src, dst, dev):
        sums[rz, what] = remote(src, dst, x_send.at[rz, what], x_recv.at[rz, what], dev)

    def x_first(rz, p):
        if rz == 2 and p == 0:
            for kind in range(2):
                give_x(rz, kind, tx.at[kind, rz, PLACE[2]], xrl.at[rz, kind], x_dev[2])
            for kind, what in ((0, 4), (1, 2)):
                give_x(rz, what, tx.at[kind, rz, PLACE[1]], xin.at[rz, 0, kind], x_dev[1])
        elif rz == 2:
            for kind, what in ((0, 3), (1, 5)):
                give_x(rz, what, tx.at[kind, rz, PLACE[3]], xin.at[rz, 1, kind], x_dev[-1])
        elif p == 0:
            give_x(rz, 0, tx.at[0, rz, PLACE[2]], xrl.at[rz, 0], x_dev[1])
            give_x(rz, 1, tx.at[1, rz, PLACE[2]], xrl.at[rz, 1], x_dev[-1])
            give_x(rz, 2, tx.at[1, rz, PLACE[1]], xin.at[rz, 0, 1], x_dev[1])
        else:
            give_x(rz, 3, tx.at[0, rz, PLACE[3]], xin.at[rz, 1, 0], x_dev[-1])

    def x_second(rz):
        for what, kind, rx, side, dev in ((0, 0, 1, 0, x_dev[1]), (1, 1, 3, 1, x_dev[-1])):
            at = PLACE[rx]
            sums[rz, what].wait_recv()
            tx[kind, rz, at] = (pf[kind, rz, at] + xrl[rz, kind].astype(F32)).astype(BF16)
            give_x(rz, 4 + kind, tx.at[kind, rz, at], xin.at[rz, side, kind], dev)

    def x_sum(rz):
        for what in (0, 1, 2, 3, 4, 5) if rz == 2 else (2, 3, 4, 5):
            sums[rz, what].wait_recv()
        for kind in range(2):
            both = xin[rz, 0, kind].astype(F32) + xin[rz, 1, kind].astype(F32)
            if rz == 2:
                both = both + xrl[rz, kind].astype(F32)
            xsum[rz, kind] = pf[kind, rz, own] + both

    def z_pass(what, src, dst, dev):
        sums[R, what] = remote(src, dst, z_send.at[what], z_recv.at[what], dev)
        late.append(sent.pop())

    def z_first(rz, what, kind, dst, dev):
        ztx[rz, kind] = xsum[rz, kind].astype(BF16)
        z_pass(what, ztx.at[rz, kind], dst, dev)

    def grad_step(rz, p):
        grad_pair(rz, p)
        x_first(rz, p)

    for rz in (2, 1, 3):
        grad_step(rz, 0)
        grad_step(rz, 1)
    grad_step(0, 0)
    x_second(1)
    grad_step(0, 1)
    x_sum(2)
    z_first(2, 0, 0, zrl.at[0], z_dev[1])
    z_first(2, 1, 1, zrl.at[1], z_dev[-1])
    x_second(3)
    x_second(0)
    x_sum(1)
    z_first(1, 2, 1, zin.at[0, 1], z_dev[1])
    x_sum(3)
    z_first(3, 3, 0, zin.at[1, 0], z_dev[-1])

    for c in range(HT // CH):
        part = slice(c * CH, (c + 1) * CH)
        grad_t = None
        for rz in range(R):
            for p in range(2):
                grads_2 = dsbuf[rz, pair_of(p), :, part].reshape(2 * T, CH)
                term = jnp.dot(kt[rz, p], grads_2, preferred_element_type=F32)
                grad_t = term if grad_t is None else grad_t + term
        for i in range(CH // T):
            h = c * (CH // T) + i
            dq_out[:, h * HD : (h + 1) * HD] = grad_t[:, i * T : (i + 1) * T].T.astype(BF16)
    dq_copy = pltpu.make_async_copy(dq_out, dq_hbm.at[0], out_sem.at[0])
    dq_copy.start()
    drain(sent)

    for what, kind, rz, side, dev in ((0, 0, 1, 0, z_dev[1]), (1, 1, 3, 1, z_dev[-1])):
        sums[R, what].wait_recv()
        ztx[rz, kind] = (xsum[rz, kind] + zrl[kind].astype(F32)).astype(BF16)
        z_pass(4 + kind, ztx.at[rz, kind], zin.at[side, kind], dev)
    x_sum(0)
    for what in (2, 3, 4, 5):
        sums[R, what].wait_recv()
    for kind, out in ((0, dk_ref), (1, dv_ref)):
        both = zin[0, kind].astype(F32) + zin[1, kind].astype(F32)
        out[0] = (xsum[0, kind] + both).astype(BF16)

    drain(late)
    dq_copy.wait()


def body(queries, keys, values, outputs, out_grad, positions, tile_flags):
    block = jax.ShapeDtypeStruct((1, T, HD), BF16)
    hbm = pl.BlockSpec(memory_space=pl.ANY)
    vmem = pl.BlockSpec(memory_space=pltpu.VMEM)
    dma = pltpu.SemaphoreType.DMA
    return pl.pallas_call(
        kernel,
        out_shape=(jax.ShapeDtypeStruct((1, T, H * HD), BF16), block, block),
        in_specs=[hbm] * 7,
        out_specs=(hbm, vmem, vmem),
        scratch_shapes=[
            pltpu.VMEM((T, H * HD), BF16),
            pltpu.VMEM((T, H * HD), BF16),
            pltpu.VMEM((T, H * HD), BF16),
            pltpu.VMEM((1, R * R * T), jnp.int32),
            pltpu.SMEM((1, 1, R * R), jnp.int32),
            pltpu.VMEM((HT, HD), BF16),
            pltpu.VMEM((HT, HD), BF16),
            pltpu.VMEM((HD, HT), BF16),
            pltpu.VMEM((HD, HT), BF16),
            pltpu.VMEM((2, R, R, T, HD), BF16),
            pltpu.VMEM((R, 2, HD, 2 * T), BF16),
            pltpu.VMEM((T, T), F32),
            pltpu.VMEM((R, R, T, T), F32),
            pltpu.VMEM((R, R, T, HT), F32),
            pltpu.VMEM((R, R, T, HT), BF16),
            pltpu.VMEM((8, HT), F32),
            pltpu.VMEM((8, HT), F32),
            pltpu.VMEM((1, HT), F32),
            pltpu.VMEM((1, HT), F32),
            pltpu.VMEM((2, R, R, T, HD), F32),
            pltpu.VMEM((2, R, R, T, HD), BF16),
            pltpu.VMEM((R, 2, T, HD), BF16),
            pltpu.VMEM((R, 2, 2, T, HD), BF16),
            pltpu.VMEM((R, 2, T, HD), F32),
            pltpu.VMEM((R, 2, T, HD), BF16),
            pltpu.VMEM((2, T, HD), BF16),
            pltpu.VMEM((2, 2, T, HD), BF16),
            pltpu.VMEM((T, H * HD), BF16),
            dma((7,)),
            dma((1,)),
            dma((2, 2, R, R)),
            dma((2, 2, R, R)),
            dma((R, 6)),
            dma((R, 6)),
            dma((6,)),
            dma((6,)),
        ],
        compiler_params=pltpu.CompilerParams(
            collective_id=0, has_side_effects=True, vmem_limit_bytes=56 * 1024 * 1024
        ),
        name="attention_backward",
    )(queries, keys, values, outputs, out_grad, positions, tile_flags)


def solution(mesh):
    sharded = P("col", "row", None)
    placed = (sharded,) * 5 + (P("col", None), sharded)
    return jax.shard_map(
        body, mesh=mesh, in_specs=placed, out_specs=(sharded,) * 3, check_vma=False
    )
```

time: 70.6 us -> 64.3 us (0.911)
  the two profiles are of different devices: /device:TPU:72 before, /device:TPU:106 now
where the time goes in v2:
time: 64.3 us; the launch traced here: 64.1 us
  Pallas kernels  60.4 us (94%)
  local copies, waits for them, and re-layouts  3.06 us (5%)
  between operations  0.65 us (1%)
    pallas_call x1, Pallas kernels, body(): pl.pallas_call(kernel, out_shape=(jax.ShapeDtypeStruct((1, T, H * HD), BF...  60.4 us
    unnamed x7, local copies, waits for them, and re-layouts  3.06 us

profile of v2, /device:TPU:106, one launch (start us, length us, event | category | flops | bytes accessed | tf_op | source)
XLA Modules:
  0.0 64.1 jit_solution(6856169557883474135)
XLA Ops:
  0.6 60.4 %attention_backward.1 = (bf16[1,128,1024]{2,1,0:T(8,128)(2,1)}, bf16[1,128,128]{2,1,0:T(8,128)(2,1)}, bf16[1,128,128]{2,1,0:T(8,128)(2,1)}) custom-call(bf16[1,128,1024]{2,1,0:T(8,128)(2,1)} %q_hbm.1, bf16[1,128,128]{2,1,0:T(8,128)(2,1)} %k_hbm.1, bf16[1,128,128]{2,1,0:T(8,128)(2,1)} %v_hbm.1, bf16[1,128,1024]{2,1,0:T(8,128)(2,1)} %o_hbm.1, ...), custom_call_target="tpu_custom_call" | custom-call | tf_op jit(solution)/shard_map/attention_backward/pallas_call | solution.py:347
  61.0 0.0 copy-start.1
  61.0 1.7 %copy.13 = bf16[1,128,1024]{2,1,0:T(8,128)(2,1)} copy(bf16[1,128,1024]{2,1,0:T(8,128)(2,1)} %get-tuple-element.6) | data formatting | bytes 524288
  62.7 0.0 copy-done.1
  62.7 0.0 copy-start
  62.7 0.6 copy.14
  63.3 0.2 copy-done
  63.5 0.6 copy.15
Async XLA Ops:
  61.0 1.7 %copy-start.1 = (bf16[1,128,128]{2,1,0:T(8,128)(2,1)S(1)}, bf16[1,128,128]{2,1,0:T(8,128)(2,1)}, u32[]{:S(2)}) copy-start(bf16[1,128,128]{2,1,0:T(8,128)(2,1)} %get-tuple-element.7) | copy-start | bytes 98308
  62.7 0.8 %copy-start = (bf16[1,128,128]{2,1,0:T(8,128)(2,1)S(1)}, bf16[1,128,128]{2,1,0:T(8,128)(2,1)}, u32[]{:S(2)}) copy-start(bf16[1,128,128]{2,1,0:T(8,128)(2,1)} %get-tuple-element.8) | copy-start | bytes 98308

commit v3 on v2

--- a/solution.py
+++ b/solution.py
@@ -107,8 +107,8 @@
         give(1, (rz, 0), (rz, 3), x_dev[1])
         give(0, (rz, 0), (rz, 1), x_dev[-1])
 
-    def onward_x(rz, kinds=(0, 1)):
-        for kind in kinds:
+    def onward_x(rz):
+        for kind in range(2):
             slot = (rz, 1 if kind else 3)
             got(kind, slot)
             give(kind, slot, (rz, 2), x_dev[-1 if kind else 1])
@@ -209,11 +209,11 @@
     give(0, (2, 0), (2, 3), x_dev[1])
     give(0, (2, 0), (2, 1), x_dev[-1])
     got(1, (2, 0))
+    give(1, (2, 0), (2, 2), x_dev[2])
     give(1, (2, 0), (2, 1), x_dev[-1])
     give(1, (2, 0), (2, 3), x_dev[1])
     all_of(0, 1)
     score_group(1)
-    onward_x(2, (1,))
     got(0, (2, 3))
     score_pair(2, 1)
     all_of(0, 2)

time: 64.3 us -> 63.3 us (0.984)
  the two profiles are of different devices: /device:TPU:106 before, /device:TPU:96 now
where the time goes in v3:
time: 63.3 us; the launch traced here: 63 us
  Pallas kernels  59.3 us (94%)
  local copies, waits for them, and re-layouts  3.06 us (5%)
  between operations  0.65 us (1%)
    pallas_call x1, Pallas kernels, body(): pl.pallas_call(kernel, out_shape=(jax.ShapeDtypeStruct((1, T, H * HD), BF...  59.3 us
    unnamed x7, local copies, waits for them, and re-layouts  3.06 us

profile of v3, /device:TPU:96, one launch (start us, length us, event | category | flops | bytes accessed | tf_op | source)
XLA Modules:
  0.0 63.0 jit_solution(4021354410425854940)
XLA Ops:
  0.6 59.3 %attention_backward.1 = (bf16[1,128,1024]{2,1,0:T(8,128)(2,1)}, bf16[1,128,128]{2,1,0:T(8,128)(2,1)}, bf16[1,128,128]{2,1,0:T(8,128)(2,1)}) custom-call(bf16[1,128,1024]{2,1,0:T(8,128)(2,1)} %q_hbm.1, bf16[1,128,128]{2,1,0:T(8,128)(2,1)} %k_hbm.1, bf16[1,128,128]{2,1,0:T(8,128)(2,1)} %v_hbm.1, bf16[1,128,1024]{2,1,0:T(8,128)(2,1)} %o_hbm.1, ...), custom_call_target="tpu_custom_call" | custom-call | tf_op jit(solution)/shard_map/attention_backward/pallas_call | solution.py:347
  59.9 0.0 copy-start.1
  60.0 1.7 %copy.13 = bf16[1,128,1024]{2,1,0:T(8,128)(2,1)} copy(bf16[1,128,1024]{2,1,0:T(8,128)(2,1)} %get-tuple-element.6) | data formatting | bytes 524288
  61.6 0.0 copy-done.1
  61.6 0.0 copy-start
  61.6 0.6 copy.14
  62.3 0.2 copy-done
  62.4 0.6 copy.15
Async XLA Ops:
  59.9 1.7 %copy-start.1 = (bf16[1,128,128]{2,1,0:T(8,128)(2,1)S(1)}, bf16[1,128,128]{2,1,0:T(8,128)(2,1)}, u32[]{:S(2)}) copy-start(bf16[1,128,128]{2,1,0:T(8,128)(2,1)} %get-tuple-element.7) | copy-start | bytes 98308
  61.6 0.8 %copy-start = (bf16[1,128,128]{2,1,0:T(8,128)(2,1)S(1)}, bf16[1,128,128]{2,1,0:T(8,128)(2,1)}, u32[]{:S(2)}) copy-start(bf16[1,128,128]{2,1,0:T(8,128)(2,1)} %get-tuple-element.8) | copy-start | bytes 98308
